TPU v7x, 32 devices: a whole 2x2x4 slice. The times are simulated.
32 devices in a mesh: dp: 4 (over z), tensor: 8 (over y, x, core).
Axes of the slice: x: 2, y: 2, z: 4, core: 2. Of those that a mesh axis runs over, the one named last changes fastest.
Arguments:
- activations: bfloat16 [1024, 27648], P('dp', 'tensor'), may hold values from -6 to 6
- left_factor: float32 [216, 216], replicated, may hold values from -2 to 3, as said below
- right_factor: float32 [128, 128], replicated, may hold values from -2 to 3, as said below
- clip_scale: float32 [128, 216], replicated, may hold values from 0.5 to 3
- weight_rows: bfloat16 [27648, 5120], P('tensor'), may hold values from -0.0390625 to 0.0390625
- target: bfloat16 [1024, 5120], P('dp'), may hold values from -6 to 6
Outputs:
- grad_left: float32 [216, 216], replicated
- grad_right: float32 [128, 128], replicated
- grad_input: float32 [1024, 27648], P('dp', 'tensor')
Inputs may be any that keep to these rules, and one draw needn't show every extreme that they name: `left_factor`: the identity plus independent entries of order one over the square root of 216. `right_factor`: the identity plus independent entries of order one over the square root of 128.
All inputs are finite; a program needn't handle non-finite values.
Results may differ from a plain program's by a relative error of at most 0.007.
Values may be sent and summed in bfloat16 or wider, within the bound.
A program may use at most 128 MiB of HBM per device.

v0:
```python
import jax
import jax.numpy as jnp
from jax import lax
from jax.sharding import PartitionSpec as P


def local(activations, left_factor, right_factor, clip_scale, weight_rows, target):
    highest = lax.Precision.HIGHEST
    tok_rows = activations.shape[0]
    width_left = left_factor.shape[0]
    local_right = activations.shape[1] // width_left
    inputs = activations.reshape(tok_rows, local_right, width_left)
    moved = lax.all_to_all(inputs, "tensor", split_axis=0, concat_axis=1, tiled=True)
    mixed = jnp.einsum("tji,ik->tjk", moved.astype(jnp.float32), left_factor, precision=highest)
    rotated = jnp.einsum("jl,tjk->tlk", right_factor, mixed, precision=highest)
    bounded = jnp.tanh(rotated / clip_scale)
    clipped = (clip_scale * bounded).astype(jnp.bfloat16)
    clipped_back = lax.all_to_all(clipped, "tensor", split_axis=1, concat_axis=0, tiled=True)
    partial_out = jnp.dot(
        clipped_back.reshape(tok_rows, -1), weight_rows, preferred_element_type=jnp.float32
    )
    total = lax.psum(partial_out, "tensor")
    out_grad = (total - target.astype(jnp.float32)).astype(jnp.bfloat16)
    clipped_grad = lax.dot_general(
        out_grad, weight_rows, (((1,), (1,)), ((), ())), preferred_element_type=jnp.float32
    )
    clipped_grad = clipped_grad.reshape(tok_rows, local_right, width_left)
    grad_owned = lax.all_to_all(clipped_grad, "tensor", split_axis=0, concat_axis=1, tiled=True)
    rotated_grad = grad_owned * (1.0 - bounded * bounded)
    mixed_grad = jnp.einsum("jl,tlk->tjk", right_factor, rotated_grad, precision=highest)
    right_part = jnp.einsum("tjk,tlk->jl", mixed, rotated_grad, precision=highest)
    grad_back = lax.all_to_all(mixed_grad, "tensor", split_axis=1, concat_axis=0, tiled=True)
    input_grad = jnp.einsum("tjk,ik->tji", grad_back, left_factor, precision=highest).reshape(
        tok_rows, -1
    )
    left_part = jnp.einsum("tji,tjk->ik", inputs.astype(jnp.float32), grad_back, precision=highest)
    left_sum, right_sum = lax.psum((left_part, right_part), ("dp", "tensor"))
    return (left_sum, right_sum, input_grad)


def solution(mesh):
    placed = (P("dp", "tensor"), P(), P(), P(), P("tensor", None), P("dp", None))
    return jax.shard_map(
        local, mesh=mesh, in_specs=placed, out_specs=(P(), P(), P("dp", "tensor")), check_vma=False
    )
```

profile of v0, /device:TPU:8, one launch (start us, length us, event | category | flops | bytes accessed | tf_op | source)
XLA Modules:
  0.0 508.3 jit_solution(451690624203319944)
XLA Ops:
  7.2 0.0 all-reduce.4.cloned.1.call-start
  7.2 2.7 copy.31
  9.9 3.0 copy.32
  12.9 30.3 %all_to_all.69 = bf16[256,16,216]{2,1,0:T(8,128)(2,1)S(1)} all-to-all(bf16[256,16,216]{2,1,0:T(8,128)(2,1)} %copy.32), channel_id=1, replica_groups=mesh['dp'=4,'tensor'=8] {'tensor'}, dimensions={0} | all-to-all | bytes 3538944 | tf_op jit(solution)/shard_map/all_to_all | solution.py:13
  43.2 0.3 copy.33
  43.5 2.1 fusion.6
  45.7 4.7 multiply_convert_fusion
  50.4 4.5 copy.36
  54.9 30.1 %all_to_all.70 = bf16[32,128,216]{2,0,1:T(8,128)(2,1)S(1)} all-to-all(bf16[32,128,216]{2,0,1:T(8,128)(2,1)} %copy.36), channel_id=1, replica_groups=mesh['dp'=4,'tensor'=8] {'tensor'}, dimensions={1} | all-to-all | bytes 3538944 | tf_op jit(solution)/shard_map/all_to_all | solution.py:18
  85.0 2.6 copy.38
  87.6 5.2 %reshape.21 = bf16[256,3456]{1,0:T(8,128)(2,1)} reshape(bf16[8,32,16,216]{3,2,1,0:T(8,128)(2,1)} %copy.38) | data formatting | bytes 3538944 | tf_op jit(solution)/shard_map/reshape | solution.py:20
  92.8 18.0 %fusion.12 = f32[256,5120]{1,0:T(8,128)} fusion(bf16[256,3456]{1,0:T(8,128)(2,1)} %reshape.21, bf16[3456,5120]{1,0:T(8,128)(2,1)} %param.10), kind=kOutput, calls=%fused_computation.18 | convolution fusion | flops 9059696640 | bytes 42401792 | tf_op jit(solution)/shard_map/dot_general | solution.py:19
  110.8 91.8 %all-reduce.4.cloned.1.call-done = f32[256,5120]{1,0:T(8,128)} async-done(((f32[256,5120]{1,0:T(8,128)}), f32[256,5120]{1,0:T(8,128)}) %all-reduce.4.cloned.1.call-update) | async-done | bytes 5242896 | tf_op jit(solution)/shard_map/psum | solution.py:22
  202.6 19.4 %fusion.1 = f32[256,3456]{0,1:T(8,128)} fusion(bf16[3456,5120]{1,0:T(8,128)(2,1)} %param.10, f32[256,5120]{1,0:T(8,128)} %all-reduce.4.cloned.1.call-done, bf16[256,5120]{1,0:T(8,128)(2,1)} %param.11), kind=kOutput, calls=%fused_computation.5 | convolution fusion | flops 9063628800 | bytes 46792704 | tf_op jit(solution)/shard_map/dot_general | solution.py:24
  222.0 5.3 %copy.40 = f32[256,16,216]{2,1,0:T(8,128)} copy(f32[256,16,216]{0,2,1:T(8,128)} %bitcast.63) | data formatting | bytes 7077888 | tf_op jit(solution)/shard_map/reshape | solution.py:27
  227.3 52.6 %all_to_all.71 = f32[256,16,216]{2,1,0:T(8,128)S(1)} all-to-all(f32[256,16,216]{2,1,0:T(8,128)} %copy.40), channel_id=1, replica_groups=mesh['dp'=4,'tensor'=8] {'tensor'}, dimensions={0} | all-to-all | bytes 7077888 | tf_op jit(solution)/shard_map/all_to_all | solution.py:28
  279.9 2.7 copy.41
  282.6 5.5 %copy.42 = f32[32,128,216]{1,2,0:T(8,128)} copy(f32[32,128,216]{2,1,0:T(8,128)} %bitcast.55) | data formatting | bytes 7077888 | tf_op jit(solution)/shard_map/all_to_all | solution.py:28
  288.1 6.4 %convolution_bitcast_fusion = f32[32,128,216]{1,2,0:T(8,128)} fusion(f32[32,128,216]{1,2,0:T(8,128)} %copy.42, f32[32,128,216]{1,2,0:T(8,128)} %get-tuple-element.15, f32[128,128]{1,0:T(8,128)S(1)} %copy-done.2), kind=kOutput, calls=%fused_computation.6 | convolution fusion | flops 1361608704 | bytes 10682368 | tf_op jit(solution)/shard_map/jl,tlk->tjk/dot_general | solution.py:30
  294.5 5.3 %copy.43 = f32[32,128,216]{2,0,1:T(8,128)} copy(f32[32,128,216]{1,2,0:T(8,128)} %convolution_bitcast_fusion) | data formatting | bytes 7077888 | tf_op jit(solution)/shard_map/jl,tlk->tjk/transpose | solution.py:30
  299.7 4.6 all-to-all-start.3
  304.3 0.3 all-reduce.6.cloned.1.call-start
  304.5 10.7 %fusion.3 = f32[128,128]{1,0:T(8,128)} fusion(f32[32,128,216]{1,2,0:T(8,128)} %copy-done.1, f32[32,128,216]{1,2,0:T(8,128)} %copy.42, f32[32,128,216]{1,2,0:T(8,128)} %get-tuple-element.15), kind=kOutput, calls=%fused_computation.9 | convolution fusion | flops 1361608704 | bytes 10682368 | tf_op jit(solution)/shard_map/tjk,tlk->jl/dot_general | solution.py:31
  315.3 38.1 %all-to-all-done.3 = f32[32,128,216]{2,0,1:T(8,128)} async-done(((f32[32,128,216]{2,0,1:T(8,128)}), f32[32,128,216]{2,0,1:T(8,128)}, u32[]{:S(2)}, u32[]{:S(2)}) %all-to-all-start.3) | async-done | bytes 3538976 | tf_op jit(solution)/shard_map/all_to_all | solution.py:32
  353.4 6.5 %copy.45 = f32[8,32,16,216]{3,2,1,0:T(8,128)} copy(f32[8,32,16,216]{3,1,2,0:T(8,128)} %bitcast.17) | data formatting | bytes 7077888 | tf_op jit(solution)/shard_map/all_to_all | solution.py:32
  359.9 5.1 %copy.46 = f32[256,16,216]{0,2,1:T(8,128)} copy(f32[256,16,216]{2,1,0:T(8,128)} %bitcast.56) | data formatting | bytes 7077888 | tf_op jit(solution)/shard_map/all_to_all | solution.py:32
  365.0 4.6 convolution_bitcast_fusion.1
  369.6 7.1 %fusion.4 = f32[256,16,216]{0,2,1:T(8,128)} fusion(f32[256,16,216]{0,2,1:T(8,128)} %copy.46, f32[216,216]{1,0:T(8,128)S(1)} %copy-done), kind=kOutput, calls=%fused_computation.10 | convolution fusion | flops 2293235712 | bytes 7264512 | tf_op jit(solution)/shard_map/tjk,ik->tji/dot_general | solution.py:33
  376.7 5.2 %copy.49 = f32[256,3456]{1,0:T(8,128)} copy(f32[256,3456]{0,1:T(8,128)} %bitcast.59) | data formatting | bytes 7077888
  381.9 116.3 %all-reduce.6.cloned.1.call-done = (f32[216,216]{0,1:T(8,128)}, f32[128,128]{1,0:T(8,128)}) async-done(((f32[216,216]{0,1:T(8,128)}, f32[128,128]{1,0:T(8,128)}), (f32[216,216]{0,1:T(8,128)}, f32[128,128]{1,0:T(8,128)})) %all-reduce.6.cloned.1.call-update) | async-done | bytes 252176 | tf_op jit(solution)/shard_map/psum | solution.py:37
  498.2 1.7 copy.48
  499.9 1.5 copy.59
  (10 shorter events, 0.1 us)
Async XLA Ops:
  7.2 36.4 %copy-start = (f32[216,216]{1,0:T(8,128)S(1)}, f32[216,216]{1,0:T(8,128)}, u32[]{:S(2)}) copy-start(f32[216,216]{1,0:T(8,128)} %param.7) | copy-start | bytes 559876
  7.2 195.4 %all-reduce.4.cloned.1.call-start = ((), (), s32[]{:S(2)}) async-start(), calls=%async_computation.4 | async-start | bytes 10485760 | tf_op jit(solution)/shard_map/psum | solution.py:22
  43.5 2.2 copy-start.2
  43.5 2.2 copy-start.3
  45.7 4.7 copy-start.1
  299.7 53.7 %all-to-all-start.3 = ((f32[32,128,216]{2,0,1:T(8,128)}), f32[32,128,216]{2,0,1:T(8,128)}, u32[]{:S(2)}, u32[]{:S(2)}) async-start(f32[32,128,216]{2,0,1:T(8,128)} %copy.43), calls=%async_computation.3 | async-start | bytes 8388608 | tf_op jit(solution)/shard_map/all_to_all | solution.py:32
  304.3 193.9 %all-reduce.6.cloned.1.call-start = ((), (), s32[]{:S(2)}) async-start(), calls=%async_computation.5 | async-start | bytes 573440 | tf_op jit(solution)/shard_map/psum | solution.py:37
Sparse Core Ops, SparseCore 0:
  110.9 91.6 all-reduce.3
  369.7 128.4 all-reduce.5
where the time goes:
time: 510 us; the launch traced here: 508 us
  waiting for transfers between devices  246 us (48%)
  blocking collectives  113 us (22%)
  matrix products  72.9 us (14%)
  local copies, waits for them, and re-layouts  57 us (11%)
  between operations  14.1 us (3%)
    psum x1, waiting for transfers between devices, local(): left_sum, right_sum = lax.psum((left_part, right_part), ('dp', 'tensor'))  116 us
    psum x1, waiting for transfers between devices, local(): total = lax.psum(partial_out, 'tensor')  91.8 us
    all_to_all x1, blocking collectives, local(): lax.all_to_all(clipped_grad, 'tensor', split_axis=0, concat_axis=1, tiled...  52.6 us
    all_to_all x1, waiting for transfers between devices, local(): lax.all_to_all(mixed_grad, 'tensor', split_axis=1, concat_axis=0, tiled=T...  38.1 us
    all_to_all x1, blocking collectives, local(): lax.all_to_all(inputs, 'tensor', split_axis=0, concat_axis=1, tiled=True)  30.3 us
    all_to_all x1, blocking collectives, local(): lax.all_to_all(clipped, 'tensor', split_axis=1, concat_axis=0, tiled=True)  30.1 us
    dot_general x1, matrix products, local(): lax.dot_general(out_grad, weight_rows, (((1,), (1,)), ((), ())), preferre...  19.4 us
    dot_general x1, matrix products, local(): jnp.dot(clipped_back.reshape(tok_rows, -1), weight_rows, preferred_elemen...  18 us
  transfers between devices with their start and end apart: 3, of which 3 were waited for; matrix products, arithmetic and copies ran while one was open for 5% of the time, Pallas kernels for 0%

commit v1 on v0

--- a/solution.py
+++ b/solution.py
@@ -19,7 +19,7 @@
     partial_out = jnp.dot(
         clipped_back.reshape(tok_rows, -1), weight_rows, preferred_element_type=jnp.float32
     )
-    total = lax.psum(partial_out, "tensor")
+    total = jnp.sum(lax.all_gather(partial_out, axis_name="tensor"), 0)
     out_grad = (total - target.astype(jnp.float32)).astype(jnp.bfloat16)
     clipped_grad = lax.dot_general(
         out_grad, weight_rows, (((1,), (1,)), ((), ())), preferred_element_type=jnp.float32

time: 510 us -> 632 us (1.24)
  waiting for transfers between devices: 246 us -> 351 us
  other arithmetic: 0 us -> 18.1 us
    all_gather x0 -> x1, waiting for transfers between devices: none -> 196 us  [local(): total = jnp.sum(lax.all_gather(partial_out, axis_name='tensor'), 0)]
    psum x1 -> x0, waiting for transfers between devices: 91.8 us -> none  [local(): total = lax.psum(partial_out, 'tensor')]
    reduce_sum x0 -> x1, other arithmetic: none -> 18.1 us  [local(): total = jnp.sum(lax.all_gather(partial_out, axis_name='tensor'), 0)]
  transfers between devices with their start and end apart: 3 -> 3, of which waited for: 3 -> 3; matrix products, arithmetic and copies ran while one was open for 5% -> 4% of each run, Pallas kernels for 0% -> 0%
where the time goes in v1:
time: 632 us; the launch traced here: 631 us
  waiting for transfers between devices  351 us (56%)
  blocking collectives  113 us (18%)
  matrix products  72.9 us (12%)
  local copies, waits for them, and re-layouts  57 us (9%)
  other arithmetic  18.1 us (3%)
  between operations  14.1 us (2%)
    all_gather x1, waiting for transfers between devices, local(): total = jnp.sum(lax.all_gather(partial_out, axis_name='tensor'), 0)  196 us
    psum x1, waiting for transfers between devices, local(): left_sum, right_sum = lax.psum((left_part, right_part), ('dp', 'tensor'))  116 us
    all_to_all x1, blocking collectives, local(): lax.all_to_all(clipped_grad, 'tensor', split_axis=0, concat_axis=1, tiled...  52.6 us
    all_to_all x1, waiting for transfers between devices, local(): lax.all_to_all(mixed_grad, 'tensor', split_axis=1, concat_axis=0, tiled=T...  38.3 us
    all_to_all x1, blocking collectives, local(): lax.all_to_all(inputs, 'tensor', split_axis=0, concat_axis=1, tiled=True)  30.3 us
    all_to_all x1, blocking collectives, local(): lax.all_to_all(clipped, 'tensor', split_axis=1, concat_axis=0, tiled=True)  30.1 us
    dot_general x1, matrix products, local(): lax.dot_general(out_grad, weight_rows, (((1,), (1,)), ((), ())), preferre...  19.4 us
    reduce_sum x1, other arithmetic, local(): total = jnp.sum(lax.all_gather(partial_out, axis_name='tensor'), 0)  18.1 us
  transfers between devices with their start and end apart: 3, of which 3 were waited for; matrix products, arithmetic and copies ran while one was open for 4% of the time, Pallas kernels for 0%

profile of v1, /device:TPU:8, one launch (start us, length us, event | category | flops | bytes accessed | tf_op | source)
XLA Modules:
  0.0 630.9 jit_solution(16488020578709377023)
XLA Ops:
  7.2 2.7 copy.31
  9.9 3.0 copy.32
  12.9 30.3 %all_to_all.69 = bf16[256,16,216]{2,1,0:T(8,128)(2,1)S(1)} all-to-all(bf16[256,16,216]{2,1,0:T(8,128)(2,1)} %copy.32), channel_id=1, replica_groups=mesh['dp'=4,'tensor'=8] {'tensor'}, dimensions={0} | all-to-all | bytes 3538944 | tf_op jit(solution)/shard_map/all_to_all | solution.py:13
  43.2 0.3 copy.33
  43.5 2.1 fusion.6
  45.7 4.7 multiply_convert_fusion
  50.4 4.5 copy.36
  54.9 30.1 %all_to_all.70 = bf16[32,128,216]{2,0,1:T(8,128)(2,1)S(1)} all-to-all(bf16[32,128,216]{2,0,1:T(8,128)(2,1)} %copy.36), channel_id=1, replica_groups=mesh['dp'=4,'tensor'=8] {'tensor'}, dimensions={1} | all-to-all | bytes 3538944 | tf_op jit(solution)/shard_map/all_to_all | solution.py:18
  85.0 2.6 copy.38
  87.6 5.1 reshape.21
  92.7 18.0 %fusion.12 = f32[256,5120]{1,0:T(8,128)} fusion(bf16[256,3456]{1,0:T(8,128)(2,1)} %reshape.21, bf16[3456,5120]{1,0:T(8,128)(2,1)} %param.10), kind=kOutput, calls=%fused_computation.18 | convolution fusion | flops 9059696640 | bytes 42401792 | tf_op jit(solution)/shard_map/dot_general | solution.py:19
  110.8 196.4 %all-gather.3.cloned.1.call-done = f32[2048,5120]{1,0:T(8,128)} async-done(((f32[256,5120]{1,0:T(8,128)}), f32[2048,5120]{1,0:T(8,128)}) %all-gather.3.cloned.1.call-update) | async-done | bytes 41943056 | tf_op jit(solution)/shard_map/all_gather | solution.py:22
  307.2 18.1 %reduce_sum.9 = f32[256,5120]{1,0:T(8,128)} reduce(f32[8,256,5120]{2,1,0:T(8,128)} %bitcast.55, f32[]{:T(128)} %constant.0.clone.1), dimensions={0}, to_apply=%region_0.0 | reduce | flops 9175040 | bytes 47185924 | tf_op jit(solution)/shard_map/reduce_sum | solution.py:22
  325.3 19.4 %fusion.1 = f32[256,3456]{0,1:T(8,128)} fusion(bf16[3456,5120]{1,0:T(8,128)(2,1)} %param.10, f32[256,5120]{1,0:T(8,128)} %reduce_sum.9, bf16[256,5120]{1,0:T(8,128)(2,1)} %param.11), kind=kOutput, calls=%fused_computation.5 | convolution fusion | flops 9063628800 | bytes 46792704 | tf_op jit(solution)/shard_map/dot_general | solution.py:24
  344.7 5.3 copy.40
  350.0 52.6 %all_to_all.71 = f32[256,16,216]{2,1,0:T(8,128)S(1)} all-to-all(f32[256,16,216]{2,1,0:T(8,128)} %copy.40), channel_id=1, replica_groups=mesh['dp'=4,'tensor'=8] {'tensor'}, dimensions={0} | all-to-all | bytes 7077888 | tf_op jit(solution)/shard_map/all_to_all | solution.py:28
  402.7 2.6 copy.41
  405.3 5.4 copy.42
  410.7 6.3 %convolution_bitcast_fusion = f32[32,128,216]{1,2,0:T(8,128)} fusion(f32[32,128,216]{1,2,0:T(8,128)} %copy.42, f32[32,128,216]{1,2,0:T(8,128)} %get-tuple-element.15, f32[128,128]{1,0:T(8,128)S(1)} %copy-done.2), kind=kOutput, calls=%fused_computation.6 | convolution fusion | flops 1361608704 | bytes 10682368 | tf_op jit(solution)/shard_map/jl,tlk->tjk/dot_general | solution.py:30
  417.1 5.3 copy.43
  422.3 4.6 all-to-all-start.3
  426.9 0.0 all-reduce.3.cloned.1.call-start
  426.9 10.7 %fusion.3 = f32[128,128]{1,0:T(8,128)} fusion(f32[32,128,216]{1,2,0:T(8,128)} %copy-done.1, f32[32,128,216]{1,2,0:T(8,128)} %copy.42, f32[32,128,216]{1,2,0:T(8,128)} %get-tuple-element.15), kind=kOutput, calls=%fused_computation.9 | convolution fusion | flops 1361608704 | bytes 10682368 | tf_op jit(solution)/shard_map/tjk,tlk->jl/dot_general | solution.py:31
  437.7 38.3 %all-to-all-done.3 = f32[32,128,216]{2,0,1:T(8,128)} async-done(((f32[32,128,216]{2,0,1:T(8,128)}), f32[32,128,216]{2,0,1:T(8,128)}, u32[]{:S(2)}, u32[]{:S(2)}) %all-to-all-start.3) | async-done | bytes 3538976 | tf_op jit(solution)/shard_map/all_to_all | solution.py:32
  476.0 6.6 %copy.45 = f32[8,32,16,216]{3,2,1,0:T(8,128)} copy(f32[8,32,16,216]{3,1,2,0:T(8,128)} %bitcast.18) | data formatting | bytes 7077888 | tf_op jit(solution)/shard_map/all_to_all | solution.py:32
  482.6 5.1 copy.46
  487.7 4.6 convolution_bitcast_fusion.1
  492.3 7.1 %fusion.4 = f32[256,16,216]{0,2,1:T(8,128)} fusion(f32[256,16,216]{0,2,1:T(8,128)} %copy.46, f32[216,216]{1,0:T(8,128)S(1)} %copy-done), kind=kOutput, calls=%fused_computation.10 | convolution fusion | flops 2293235712 | bytes 7264512 | tf_op jit(solution)/shard_map/tjk,ik->tji/dot_general | solution.py:33
  499.4 5.2 copy.49
  504.5 116.3 %all-reduce.3.cloned.1.call-done = (f32[216,216]{0,1:T(8,128)}, f32[128,128]{1,0:T(8,128)}) async-done(((f32[216,216]{0,1:T(8,128)}, f32[128,128]{1,0:T(8,128)}), (f32[216,216]{0,1:T(8,128)}, f32[128,128]{1,0:T(8,128)})) %all-reduce.3.cloned.1.call-update) | async-done | bytes 252176 | tf_op jit(solution)/shard_map/psum | solution.py:37
  620.9 1.7 copy.48
  622.6 1.5 copy.58
  (11 shorter events, 0.1 us)
Async XLA Ops:
  7.2 36.4 %copy-start = (f32[216,216]{1,0:T(8,128)S(1)}, f32[216,216]{1,0:T(8,128)}, u32[]{:S(2)}) copy-start(f32[216,216]{1,0:T(8,128)} %param.7) | copy-start | bytes 559876
  7.2 300.0 %all-gather.3.cloned.1.call-start = ((), (), s32[]{:S(2)}) async-start(), calls=%async_computation.4 | async-start | bytes 47185920 | tf_op jit(solution)/shard_map/all_gather | solution.py:22
  43.5 2.2 copy-start.2
  43.5 2.2 copy-start.3
  45.7 4.7 copy-start.1
  422.3 53.7 %all-to-all-start.3 = ((f32[32,128,216]{2,0,1:T(8,128)}), f32[32,128,216]{2,0,1:T(8,128)}, u32[]{:S(2)}, u32[]{:S(2)}) async-start(f32[32,128,216]{2,0,1:T(8,128)} %copy.43), calls=%async_computation.3 | async-start | bytes 8388608 | tf_op jit(solution)/shard_map/all_to_all | solution.py:32
  426.9 194.0 %all-reduce.3.cloned.1.call-start = ((), (), s32[]{:S(2)}) async-start(), calls=%async_computation.5 | async-start | bytes 573440 | tf_op jit(solution)/shard_map/psum | solution.py:37
Sparse Core Ops, SparseCore 0:
  110.9 196.2 all-gather.2
  492.4 128.4 all-reduce.2
